TPU v7x, 32 devices: a whole 2x2x4 slice. The times are simulated.
32 devices in a mesh: member: 2 (over x), lon: 8 (over z, y), lat: 2 (over core).
Axes of the slice: x: 2, y: 2, z: 4, core: 2. Of those that a mesh axis runs over, the one named last changes fastest.
Arguments:
- strain_rate: float32 [3, 256, 2160], P(None, 'lon', 'lat'), may hold values from -6 to 6
- stress_start: float32 [3, 256, 2160], P(None, 'lon', 'lat'), may hold values from -3 to 3
- concentration: float32 [256, 2160], P('lon', 'lat'), may hold values from 0.5 to 1
- cell_class: int32 [512, 2160], P(('member', 'lon'), 'lat'), parts along dimension 0, may hold values from 0 to 7
- land_mask: int32 [256, 2160], P('lon', 'lat'), may hold values 0 or 1
- fold_partner: int32 [256], replicated, may hold values from 0 to 255, each once
- kernel_weights: float32 [7, 7], replicated, may hold values from 0.05 to 0.5
Outputs:
- stress_out: float32 [3, 512, 2160], P(None, ('member', 'lon'), 'lat'), parts along dimension 1
- damage_out: float32 [512, 2160], P(('member', 'lon'), 'lat'), parts along dimension 0
- mean_overstress: float32 [6], P('member'), parts along dimension 0
There are 2 independent parts, one for each index of `member`. A program takes and returns all parts, laid end to end along the dimension named above; an argument that names none is the same for every part. Nothing has to cross between parts.
Inputs may be any that keep to these rules, and one draw needn't show every extreme that they name: `fold_partner`: each of the 256 longitude indices appears once.
All inputs are finite; a program needn't handle non-finite values. No bound on the sum of `land_mask` on one device may be relied on, other than what follows from the above.
Results may differ from a plain program's by a relative error of at most 0.0001.
Values sent between devices are 32-bit elements; how exact they have to be, the bound alone decides.
A program may use at most 64 MiB of HBM per device.

v0:
```python
import functools

import jax
import jax.numpy as jnp
from jax import lax
from jax.experimental import pallas as pl
from jax.experimental.pallas import tpu as pltpu
from jax.sharding import PartitionSpec as P

ITERS = 3
LANES = 128
SUB = 8
NORTH = 66
MESH = pl.DeviceIdType.MESH
F32 = jnp.float32


def kernel(
    nlon, nlat, nrows, R, L, side,
    w_hbm, partner_hbm, e_hbm, s_hbm, conc_hbm, class_hbm, mask_hbm,
    stress_ref, damage_ref, mean_ref,
    w_ref, partner_ref, where_ref,
    Z, Y, X, load, base, ocean, orl, half_ocean, half_rden, state,
    rows_out, rows_in, fixed_out, fixed_in, fixed_rows, HQ, WR, WC, C, rden_rows,
    slab, lat_in, fold_in, tops, D, T, stat, stat_in, stage,
    e_ref, s_ref, conc_ref, class_ref, mask_ref,
    in_sem, fixed_send, fixed_recv, row_send, row_recv, slab_send, lat_recv, fold_recv, stat_send, stat_recv,
):
    width = side // 2
    n = nlon * nlat
    ncols = R * SUB
    tiles = L // LANES
    lon, lat = lax.axis_index("lon"), lax.axis_index("lat")
    member = lax.axis_index("member")
    is_last = lat == nlat - 1
    me = lon * nlat + lat
    nb = nrows - (L - LANES)

    def dev(a, b):
        return (member, a, b)

    def peer(d):
        other = lax.rem(me + d, n)
        return dev(other // nlat, lax.rem(other, nlat))

    def every(first, last, body):
        if last - first <= 16:
            for d in range(first, last):
                body(d)
        else:
            lax.fori_loop(first, last, lambda d, c: (body(d), c)[1], 0)

    def tile(x, t):
        return x[:, t * LANES : (t + 1) * LANES]

    right, left = lax.rem(lon + 1, nlon), lax.rem(lon + nlon - 1, nlon)
    other_lat = lax.rem(lat + 1, nlat)

    loads = [
        pltpu.make_async_copy(a, b, in_sem.at[k])
        for k, (a, b) in enumerate((
            (mask_hbm, mask_ref), (conc_hbm, conc_ref), (class_hbm, class_ref), (s_hbm, s_ref), (e_hbm, e_ref),
            (w_hbm, w_ref), (partner_hbm, partner_ref),
        ))
    ]
    for copy in loads:
        copy.start()
    barrier = pltpu.get_barrier_semaphore()
    every(1, n, lambda d: pl.semaphore_signal(barrier, inc=1, device_id=peer(d), device_id_type=MESH))

    sub = lax.broadcasted_iota(jnp.int32, (SUB, LANES), 0)
    sub_wide = lax.broadcasted_iota(jnp.int32, (SUB, L), 0)
    lane = lax.broadcasted_iota(jnp.int32, (SUB, LANES), 1)
    slot = lax.rem(lane, width)
    packed_slot = lax.rem(lax.rem(lane, 16), width)

    edge = jnp.zeros((SUB, LANES), F32)
    for r in range(R):
        for ref in (base.at[r], ocean.at[r], orl.at[r], *(load.at[k, r] for k in range(3)), Z.at[0, r],
                    *(state.at[k, r] for k in range(3))):
            ref[:, L - LANES :] = edge
    for t in range(tiles):
        for it in range(ITERS):
            rows_in[it, t, SUB * width :, :] = edge
        fixed_rows[t] = edge
    mean_ref[...] = edge
    for copy in loads[5:]:
        copy.wait()
    for d in range(width):
        for b in range(side):
            WR[d * side + b] = jnp.where(sub < 4, w_ref[d, b], w_ref[side - 1 - d, b])
    span_lanes = 5 * width
    for d in range(1, width + 1):
        keep = (slot >= width - d) & ((lane < span_lanes) | ((lane >= NORTH) & (lane < NORTH + span_lanes)))
        for a in range(side):
            WC[(d - 1) * side + a] = jnp.where(
                keep, jnp.where(lane < NORTH - width, w_ref[a, width - d], w_ref[a, width + d]), 0.0
            )
    for i in range(ncols + 2 * width):
        p = partner_ref[lax.rem(lon * ncols + i - width + nlon * ncols, nlon * ncols)]
        col = lax.rem(p, ncols)
        where_ref[i] = ((p // ncols) * R + lax.rem(col, R)) * SUB + col // R
    for copy in loads[:5]:
        copy.wait()

    span = [min(LANES, nrows - t * LANES) for t in range(tiles)]
    sources = (
        mask_ref, conc_ref, class_ref, s_ref.at[0], s_ref.at[1], s_ref.at[2], e_ref.at[0], e_ref.at[1], e_ref.at[2]
    )
    count = jnp.zeros((SUB, LANES), F32)
    for t in range(tiles):
        cut = slice(t * LANES, t * LANES + span[t])
        for k, source in enumerate(sources):
            stage[k, t, :, : span[t]] = source[:, cut].astype(F32)
        for r in range(R):
            oc, conc, grade, s1, s2, s3, one, two, shear = (
                stage[k, t, pl.ds(r, SUB, stride=R), :][:, : span[t]] for k in range(9)
            )
            ocean[r, :, cut] = oc
            base[r, :, cut] = conc * jnp.exp(-2.0 * (1.0 - conc))
            orl[r, :, cut] = oc / (0.6 * conc)
            Z[0, r, :, cut] = oc * 0.1 * grade * conc
            for k, part in enumerate((s1, s2, s3)):
                state[k, r, :, cut] = oc * part
            load[0, r, :, cut] = (one + two / 3.0) / (8.0 / 9.0)
            load[1, r, :, cut] = (two + one / 3.0) / (8.0 / 9.0)
            load[2, r, :, cut] = (shear / (4.0 / 3.0)) / (8.0 / 9.0)
    for m in range(width):
        fixed_out[0, 0, m : m + 1, :] = orl[R - width + m, SUB - 1 : SUB, :]
        fixed_out[0, 1, m : m + 1, :] = ocean[R - width + m, SUB - 1 : SUB, :]
        fixed_out[1, 0, m : m + 1, :] = orl[width - 1 - m, 0:1, :]
        fixed_out[1, 1, m : m + 1, :] = ocean[width - 1 - m, 0:1, :]
    for r in range(R):
        oc = ocean[r]
        Z[8, r] = oc
        half_ocean[r] = 0.5 * oc
        for t in range(tiles):
            count = count + tile(oc, t)
    count = jnp.sum(count, axis=0, keepdims=True)

    pl.semaphore_wait(barrier, n - 1)

    def fixed_copy(k, to):
        return pltpu.make_async_remote_copy(
            src_ref=fixed_out.at[k, :, pl.ds(0, width), :], dst_ref=fixed_in.at[k, :, pl.ds(0, width), :],
            send_sem=fixed_send, recv_sem=fixed_recv, device_id=dev(to, lat), device_id_type=MESH,
        )

    def far_first(up, down):
        odd = lax.rem(lon, 2) == 1

        @pl.when(odd)
        def _():
            up()
            down()

        @pl.when(jnp.logical_not(odd))
        def _():
            down()
            up()

    far_first(lambda: fixed_copy(0, right).start(), lambda: fixed_copy(1, left).start())

    def conv(f, c):
        for r in range(R):
            X[width + r] = Z[f, r]
        for m in range(width):
            X[m] = jnp.where(sub_wide == 0, 0.0, pltpu.roll(Z[f, m + R - width], 1, 0))
            X[R + width + m] = jnp.where(sub_wide == SUB - 1, 0.0, pltpu.roll(Z[f, m], SUB - 1, 0))
        for b in range(side):
            acc = [None] * R
            for p in range(R + 2 * width):
                x = X[p]
                for r in range(R):
                    a = p - r
                    if 0 <= a < side:
                        term = w_ref[a, b] * x
                        acc[r] = term if acc[r] is None else acc[r] + term
            for r in range(R):
                moved = acc[r] if b == width else pltpu.roll(acc[r], (width - b) % L, 1)
                if b == 0:
                    Y[f, r] = moved
                else:
                    Y[f, r] = Y[f, r] + moved
        return c

    def row_terms(halos):
        for r in range(width):
            total = None
            for b in range(side):
                parts = []
                for t in range(tiles):
                    acc = None
                    for m in range(r, width):
                        term = WR[(m - r) * side + b] * halos[m][t]
                        acc = term if acc is None else acc + term
                    parts.append(acc)
                wide = jnp.concatenate(parts, axis=1)
                wide = wide if b == width else pltpu.roll(wide, (width - b) % L, 1)
                total = wide if total is None else total + wide
            yield r, total

    def row_term(p, f, t):
        cut = slice(t * LANES, (t + 1) * LANES)
        out = jnp.zeros((SUB, LANES), F32)
        if p < width:
            out = jnp.where(sub == 0, C[p, f : f + 1, cut], out)
        if R - 1 - p < width:
            out = jnp.where(sub == SUB - 1, C[R - 1 - p, 4 + f : 5 + f, cut], out)
        return out

    def flip(x, at):
        y = jnp.where(at == 0, pltpu.roll(x, LANES - (width - 1), 1), x)
        return jnp.where(at == width - 1, pltpu.roll(x, width - 1, 1), y)

    def column_term(f, p):
        at = width * f + width
        south = jnp.where(lane < width, pltpu.roll(T[0, p], (LANES - at) % LANES, 1), 0.0)
        north = jnp.where(
            (lane >= nb - width) & (lane < nb), pltpu.roll(T[1, p], (nb - width - NORTH - at) % LANES, 1), 0.0
        )
        return south, north

    def iteration(it, carry):
        excess = jnp.zeros((SUB, LANES), F32)
        for r in range(R):
            oc = ocean[r]
            damage = Z[0, r]
            keep = 1.0 - damage
            square = keep * keep
            scale = oc * square / (square + 0.5)
            bk = base[r] * keep
            el = [scale * (state[k, r] + bk * load[k, r]) for k in range(3)]
            half = (el[0] - el[1]) * 0.5
            tau = jnp.sqrt(half * half + el[2] * el[2] + 0.25)
            over = jnp.maximum((tau + 0.35 * (el[0] + el[1])) * orl[r], 1.0)
            q = 1.0 - 1.0 / over
            for t in range(tiles):
                excess = excess + (tile(over, t) - 1.0)
            Z[4, r] = keep * q
            for k in range(3):
                Z[1 + k, r] = el[k]
                Z[5 + k, r] = -(el[k] * q)
            for m in range(width):
                for f, part in enumerate((damage, *el)):
                    for t in range(tiles):
                        if r == R - width + m:
                            rows_out[it, t, SUB * m + f : SUB * m + f + 1, :] = tile(part, t)[SUB - 1 : SUB]
                        if r == width - 1 - m:
                            rows_out[it, t, SUB * m + 4 + f : SUB * m + 5 + f, :] = tile(part, t)[0:1]
        stat[it, 0:1, :] = jnp.sum(excess, axis=0, keepdims=True)
        stat[it, 1:2, :] = count

        def stat_copy(d):
            return pltpu.make_async_remote_copy(
                src_ref=stat.at[it], dst_ref=stat_in.at[it, d], send_sem=stat_send,
                recv_sem=stat_recv.at[it], device_id=peer(d), device_id_type=MESH,
            )

        every(1, n, lambda d: stat_copy(d).start())

        low = jnp.zeros((SUB, LANES), F32)
        high = jnp.zeros((SUB, LANES), F32)
        for r in range(R):
            for f in range(9):
                at = 32 * r + (width * f if f < 4 else (16 + width * (f - 4) if f < 8 else 4 * width))
                here = (lane >= at) & (lane < at + width)
                low = jnp.where(here, pltpu.roll(Z[f, r, :, :LANES], at, 1), low)
                high = jnp.where(here, pltpu.roll(Z[f, r, :, L - LANES :], (at + width - nb) % LANES, 1), high)
        slab[it, 0] = jnp.where(is_last, low, high)
        slab[it, 1] = high

        def lat_copy(k):
            to = lax.rem(lon + 1 - k + nlon, nlon)
            return pltpu.make_async_remote_copy(
                src_ref=slab.at[it, 0], dst_ref=lat_in.at[it, k], send_sem=slab_send,
                recv_sem=lat_recv.at[it], device_id=dev(to, other_lat), device_id_type=MESH,
            )

        def fold_copy(d):
            return pltpu.make_async_remote_copy(
                src_ref=slab.at[it, 1], dst_ref=fold_in.at[it, lon],
                send_sem=slab_send, recv_sem=fold_recv.at[it],
                device_id=dev(lax.rem(lon + d, nlon), lat), device_id_type=MESH,
            )

        @pl.when(is_last)
        def _():
            every(1, nlon, lambda d: fold_copy(d).start())
            fold_in[it, lon] = slab[it, 1]

        for k in range(3):
            lat_copy(k).start()

        def row_copy(s, m, to):
            piece = pl.ds(SUB * m + 4 * s, 4)
            return pltpu.make_async_remote_copy(
                src_ref=rows_out.at[it, :, piece, :], dst_ref=rows_in.at[it, :, piece, :], send_sem=row_send,
                recv_sem=row_recv.at[it], device_id=dev(to, lat), device_id_type=MESH,
            )

        def start_rows(s, to):
            for m in range(width):
                row_copy(s, m, to).start()

        far_first(lambda: start_rows(0, right), lambda: start_rows(1, left))

        lax.fori_loop(0, jnp.where(it == 0, 9, 8), conv, 0)

        def drain(ref, sem):
            pltpu.make_async_copy(ref, ref, sem).wait()

        def wait_halos():
            drain(rows_in.at[it, :, pl.ds(0, SUB * width), :], row_recv.at[it])
            drain(lat_in.at[it], lat_recv.at[it])

            @pl.when(is_last)
            def _():
                drain(fold_in.at[it, pl.ds(0, nlon - 1)], fold_recv.at[it])

        drain(stat_in.at[it, pl.ds(1, n - 1)], stat_recv.at[it])
        total = stat[it]
        if n <= 16:
            for d in range(1, n):
                total = total + stat_in[it, d]
        else:
            total = lax.fori_loop(1, n, lambda d, c: c + stat_in[it, d], total)
        sums = jnp.sum(total, axis=1, keepdims=True)
        mean = sums[0:1] / (sums[1:2] + 1.0)
        factor = 1.0 / (1.0 + 2.0 * mean)
        mean_ref[...] = jnp.where(lane == it, mean, mean_ref[...])

        def columns():
            @pl.when(is_last)
            def _():
                def spread(k):
                    got = fold_in[it, k]
                    got = got + factor * pltpu.roll(got, LANES - 16, 1)
                    for r in range(R):
                        tops[pl.ds((k * R + r) * SUB, SUB), :] = pltpu.roll(got, (NORTH - 32 * r) % LANES, 1)

                every(0, nlon, spread)
                for i in range(ncols + 2 * width):
                    D[i : i + 1, :] = tops[pl.ds(where_ref[i], 1), :]

            south_side = lane < NORTH - width
            own = []
            for k in range(3):
                got = lat_in[it, k]
                got = got + factor * pltpu.roll(got, LANES - 16, 1)
                own.append(jnp.where(is_last, got, flip(got, packed_slot)))

            def piece(k, r):
                return jnp.where(
                    is_last, pltpu.roll(own[k], (LANES - 32 * r) % LANES, 1),
                    pltpu.roll(own[k], (NORTH - 32 * r) % LANES, 1),
                )

            mid = [piece(1, r) for r in range(R)]
            ghosts = [None] * (R + 2 * width)
            for r in range(R):
                ghosts[width + r] = mid[r]
            for m in range(width):
                r = m + R - width
                ghosts[m] = jnp.where(sub == 0, pltpu.roll(piece(0, r), 1, 0), pltpu.roll(mid[r], 1, 0))
                ghosts[R + width + m] = jnp.where(
                    sub == SUB - 1, pltpu.roll(piece(2, m), SUB - 1, 0), pltpu.roll(mid[m], SUB - 1, 0)
                )
            for p in range(R + 2 * width):
                fold = D[pl.ds(p, SUB, stride=R), :]
                ghosts[p] = jnp.where(
                    south_side, jnp.where(is_last, ghosts[p], 0.0), jnp.where(is_last, fold, ghosts[p])
                )
            for r in range(R):
                total = None
                for d in range(1, width + 1):
                    acc = None
                    for a in range(side):
                        term = WC[(d - 1) * side + a] * ghosts[r + a]
                        acc = term if acc is None else acc + term
                    acc = pltpu.roll(acc, d, 1)
                    total = acc if total is None else total + acc
                T[0, r] = total
                T[1, r] = flip(total, slot)

        def finish_ocean():
            drain(fixed_in.at[:, :, pl.ds(0, width), :], fixed_recv)
            drain(fixed_in.at[:, :, pl.ds(0, width), :], fixed_send)
            for t in range(tiles):
                cut = slice(t * LANES, (t + 1) * LANES)
                for m in range(width):
                    for s in range(2):
                        fixed_rows[t, 2 * m + s : 2 * m + s + 1, :] = fixed_in[s, 0, m : m + 1, cut]
            halos = [
                [
                    jnp.where(
                        sub < 4, fixed_in[0, 1, m : m + 1, t * LANES : (t + 1) * LANES],
                        fixed_in[1, 1, m : m + 1, t * LANES : (t + 1) * LANES],
                    )
                    for t in range(tiles)
                ]
                for m in range(width)
            ]
            for r, total in row_terms(halos):
                C[r] = total
            for r in range(R):
                south, north = column_term(4, r)
                for t in range(tiles):
                    cut = slice(t * LANES, (t + 1) * LANES)
                    denom = Y[8, r, :, cut] + row_term(r, 0, t)
                    if t == 0:
                        denom = denom + south
                    if t == tiles - 1:
                        denom = denom + north
                    half_rden[r, :, cut] = half_ocean[r, :, cut] / (denom + 1.0)
            for r in range(width):
                rden_rows[r] = jnp.where(
                    sub_wide < 4, half_rden[r, 0:1, :], half_rden[R - 1 - r, SUB - 1 : SUB, :]
                )

        @pl.when(it == 0)
        def _():
            wait_halos()
            columns()
            finish_ocean()

        for r in range(R):
            for t in range(tiles):
                cut = slice(t * LANES, (t + 1) * LANES)
                ho, hr = half_ocean[r, :, cut], half_rden[r, :, cut]
                for f in range(4):
                    local = Z[f, r, :, cut] + factor * Z[4 + f, r, :, cut]
                    spread_out = Y[f, r, :, cut] + factor * Y[4 + f, r, :, cut]
                    fresh = ho * local + hr * spread_out
                    if f == 0:
                        Z[0, r, :, cut] = fresh
                    else:
                        state[f - 1, r, :, cut] = fresh

        @pl.when(it > 0)
        def _():
            wait_halos()
            columns()

        for t in range(tiles):
            e = [rows_in[it, t, pl.ds(k, SUB, stride=4), :] for k in range(1, 4)]
            half = (e[0] - e[1]) * 0.5
            tau = jnp.sqrt(half * half + e[2] * e[2] + 0.25)
            over = jnp.maximum((tau + 0.35 * (e[0] + e[1])) * fixed_rows[t], 1.0)
            HQ[t] = factor * (1.0 - 1.0 / over)
        halos = [[None] * tiles for _ in range(width)]
        head = (sub == 0) | (sub == 4)
        for m in range(width):
            for t in range(tiles):
                fq = jnp.where(sub < 4, HQ[t, 2 * m : 2 * m + 1, :], HQ[t, 2 * m + 1 : 2 * m + 2, :])
                raw = rows_in[it, t, SUB * m : SUB * (m + 1), :]
                halos[m][t] = raw * (1.0 - fq) + jnp.where(head, fq, 0.0)
        for r, total in row_terms(halos):
            C[r] = total * rden_rows[r]
        for f in range(4):
            for r in range(R):
                into = Z.at[0, r] if f == 0 else state.at[f - 1, r]
                south, north = column_term(f, r)
                for t in range(tiles):
                    cut = slice(t * LANES, (t + 1) * LANES)
                    add = row_term(r, f, t)
                    if t == 0:
                        add = add + half_rden[r, :, cut] * south
                    if t == tiles - 1:
                        add = add + half_rden[r, :, cut] * north
                    into[:, cut] = into[:, cut] + add

        drain(stat_in.at[it, pl.ds(1, n - 1)], stat_send)
        drain(rows_out.at[it], row_send)
        drain(lat_in.at[it], slab_send)

        @pl.when(is_last)
        def _():
            drain(fold_in.at[it, pl.ds(0, nlon - 1)], slab_send)

        return carry

    lax.fori_loop(0, ITERS, iteration, 0)
    outputs = (damage_ref, stress_ref.at[0], stress_ref.at[1], stress_ref.at[2])
    for t in range(tiles):
        cut = slice(t * LANES, t * LANES + span[t])
        for k, target in enumerate(outputs):
            for r in range(R):
                value = Z[0, r, :, t * LANES : (t + 1) * LANES] if k == 0 else state[k - 1, r, :, t * LANES : (t + 1) * LANES]
                stage[k, t, pl.ds(r, SUB, stride=R), :] = value
            target[:, cut] = stage[k, t, :, : span[t]]


def write_out(stress_vmem, damage_vmem, mean_vmem, stress_hbm, damage_hbm, mean_hbm, mean_smem, sem):
    copies = [
        pltpu.make_async_copy(stress_vmem, stress_hbm, sem.at[0]),
        pltpu.make_async_copy(damage_vmem, damage_hbm, sem.at[1]),
        pltpu.make_async_copy(mean_smem, mean_hbm, sem.at[2]),
    ]
    copies[0].start()
    copies[1].start()
    row = mean_vmem[0:1, :]
    for k in range(ITERS):
        mean_smem[k] = row[0, k]
    copies[2].start()
    for copy in copies:
        copy.wait()


def shards(nlon, nlat, strain_rate, stress_start, concentration, cell_class, land_mask, fold_partner, kernel_weights):
    ncols, nrows = concentration.shape
    side = kernel_weights.shape[0]
    width = side // 2
    R = ncols // SUB
    L = -(-(nrows + 2 * width) // LANES) * LANES
    tiles = L // LANES
    n = nlon * nlat
    V = lambda *shape: pltpu.VMEM(shape, F32)
    S = lambda *shape: pltpu.SemaphoreType.DMA(shape)
    planes = R + 2 * width
    ext = -(-(ncols + 2 * width) // SUB) * SUB
    hbm = pl.BlockSpec(memory_space=pltpu.HBM)
    vmem = pl.BlockSpec(memory_space=pltpu.VMEM)
    stress, damage, mean = pl.pallas_call(
        functools.partial(kernel, nlon, nlat, nrows, R, L, side),
        out_shape=(
            pltpu.VMEM((3, ncols, nrows), F32),
            pltpu.VMEM((ncols, nrows), F32),
            pltpu.VMEM((SUB, LANES), F32),
        ),
        in_specs=[hbm] * 7,
        out_specs=(vmem,) * 3,
        scratch_shapes=[
            pltpu.SMEM(kernel_weights.shape, F32), pltpu.SMEM(fold_partner.shape, jnp.int32),
            pltpu.SMEM((ncols + 2 * width,), jnp.int32),
            V(9, R, SUB, L), V(9, R, SUB, L), V(planes, SUB, L),
            V(3, R, SUB, L), V(R, SUB, L), V(R, SUB, L), V(R, SUB, L), V(R, SUB, L), V(R, SUB, L), V(3, R, SUB, L),
            V(ITERS, tiles, SUB * width, LANES), V(ITERS, tiles, SUB * (width + 1), LANES),
            V(2, 2, 4, L), V(2, 2, 4, L), V(tiles, SUB, LANES), V(tiles, SUB, LANES),
            V(width * side, SUB, LANES), V(width * side, SUB, LANES), V(width, SUB, L), V(width, SUB, L),
            V(ITERS, 2, SUB, LANES), V(ITERS, 3, SUB, LANES), V(ITERS, nlon, SUB, LANES),
            V(nlon * R * SUB, LANES), V(ext, LANES), V(2, R, SUB, LANES),
            V(ITERS, 2, LANES), V(ITERS, n, 2, LANES), V(9, tiles, ncols, LANES),
            V(3, ncols, nrows), V(3, ncols, nrows), V(ncols, nrows),
            pltpu.VMEM((ncols, nrows), jnp.int32), pltpu.VMEM((ncols, nrows), jnp.int32),
            S(7), pltpu.SemaphoreType.DMA, pltpu.SemaphoreType.DMA, pltpu.SemaphoreType.DMA, S(ITERS),
            pltpu.SemaphoreType.DMA, S(ITERS), S(ITERS), pltpu.SemaphoreType.DMA, S(ITERS),
        ],
        compiler_params=pltpu.CompilerParams(
            collective_id=0, has_side_effects=True, vmem_limit_bytes=67043328 - 1024 * 1024
        ),
    )(kernel_weights, fold_partner, strain_rate, stress_start, concentration, cell_class, land_mask)
    return pl.pallas_call(
        write_out,
        out_shape=(
            jax.ShapeDtypeStruct((3, ncols, nrows), F32),
            jax.ShapeDtypeStruct((ncols, nrows), F32),
            jax.ShapeDtypeStruct((ITERS,), F32),
        ),
        in_specs=[vmem] * 3,
        out_specs=(hbm,) * 3,
        scratch_shapes=[pltpu.SMEM((ITERS,), F32), S(3)],
    )(stress, damage, mean)


def solution(mesh):
    in_specs = (
        P(None, "lon", "lat"),
        P(None, "lon", "lat"),
        P("lon", "lat"),
        P(("member", "lon"), "lat"),
        P("lon", "lat"),
        P(),
        P(),
    )
    out_specs = (P(None, ("member", "lon"), "lat"), P(("member", "lon"), "lat"), P("member"))
    body = functools.partial(shards, mesh.shape["lon"], mesh.shape["lat"])
    return jax.shard_map(body, mesh=mesh, in_specs=in_specs, out_specs=out_specs, check_vma=False)
```

profile of v0, /device:TPU:1, one launch (start us, length us, event | category | flops | bytes accessed | tf_op | source)
XLA Modules:
  0.0 30.9 jit_solution(17093693304280233065)
XLA Ops:
  0.6 26.3 %shard_map.94 = (f32[3,32,1080]{2,1,0:T(8,128)S(1)}, f32[32,1080]{1,0:T(8,128)S(1)}, f32[8,128]{1,0:T(8,128)S(1)}) custom-call(f32[7,7]{1,0:T(8,128)} %w_hbm.1, s32[256]{0:T(256)} %partner_hbm.1, f32[3,32,1080]{2,1,0:T(8,128)} %e_hbm.1, f32[3,32,1080]{2,1,0:T(8,128)} %s_hbm.1, f32[32,1080]{1,0:T(8,128)} %conc_hbm.1, s32[32,1080]{1,0:T(8,128)} %class_hbm.1, ...), custom_call_target="tpu_custom_call" | custom-call | tf_op jit(solution)/shard_map/pallas_call | solution.py:524
  26.9 0.0 copy-start
  26.9 0.8 %copy-done = f32[3,32,1080]{2,1,0:T(8,128)} copy-done((f32[3,32,1080]{2,1,0:T(8,128)}, f32[3,32,1080]{2,1,0:T(8,128)S(1)}, u32[]{:S(2)}) %copy-start) | copy-done | bytes 414744
  27.7 0.0 copy-start.1
  27.7 0.7 %copy-done.1 = f32[32,1080]{1,0:T(8,128)} copy-done((f32[32,1080]{1,0:T(8,128)}, f32[32,1080]{1,0:T(8,128)S(1)}, u32[]{:S(2)}) %copy-start.1) | copy-done | bytes 138264
  28.3 0.0 copy-start.2
  28.3 0.6 %copy-done.2 = f32[8,128]{1,0:T(8,128)} copy-done((f32[8,128]{1,0:T(8,128)}, f32[8,128]{1,0:T(8,128)S(1)}, u32[]{:S(2)}) %copy-start.2) | copy-done | bytes 4120
  28.9 1.9 %shard_map.95 = (f32[3,32,1080]{2,1,0:T(8,128)}, f32[32,1080]{1,0:T(8,128)}, f32[3]{0:T(128)}) custom-call(f32[3,32,1080]{2,1,0:T(8,128)} %copy-done, f32[32,1080]{1,0:T(8,128)} %copy-done.1, f32[8,128]{1,0:T(8,128)} %copy-done.2), custom_call_target="tpu_custom_call" | custom-call | tf_op jit(solution)/shard_map/pallas_call | solution.py:553
Async XLA Ops:
  26.9 0.8 %copy-start = (f32[3,32,1080]{2,1,0:T(8,128)}, f32[3,32,1080]{2,1,0:T(8,128)S(1)}, u32[]{:S(2)}) copy-start(f32[3,32,1080]{2,1,0:T(8,128)S(1)} %get-tuple-element.6.stress_vmem) | copy-start | bytes 1244164
  27.7 0.7 %copy-start.1 = (f32[32,1080]{1,0:T(8,128)}, f32[32,1080]{1,0:T(8,128)S(1)}, u32[]{:S(2)}) copy-start(f32[32,1080]{1,0:T(8,128)S(1)} %get-tuple-element.7.damage_vmem) | copy-start | bytes 414724
  28.3 0.6 %copy-start.2 = (f32[8,128]{1,0:T(8,128)}, f32[8,128]{1,0:T(8,128)S(1)}, u32[]{:S(2)}) copy-start(f32[8,128]{1,0:T(8,128)S(1)} %get-tuple-element.8.mean_vmem) | copy-start | bytes 12292
where the time goes:
time: 31.2 us; the launch traced here: 30.9 us
  Pallas kernels  28.2 us (90%)
  local copies, waits for them, and re-layouts  1.99 us (6%)
  between operations  0.65 us (2%)
    pallas_call x1, Pallas kernels, shards(): pl.pallas_call(functools.partial(kernel, nlon, nlat, nrows, R, L, side),...  26.3 us
    unnamed x6, local copies, waits for them, and re-layouts  1.99 us
    pallas_call x1, Pallas kernels, shards(): pl.pallas_call(write_out, out_shape=(jax.ShapeDtypeStruct((3, ncols, nrow...  1.93 us

commit v1 on v0

--- a/solution.py
+++ b/solution.py
@@ -100,36 +100,63 @@
         p = partner_ref[lax.rem(lon * ncols + i - width + nlon * ncols, nlon * ncols)]
         col = lax.rem(p, ncols)
         where_ref[i] = ((p // ncols) * R + lax.rem(col, R)) * SUB + col // R
-    for copy in loads[:5]:
+    span = [min(LANES, nrows - t * LANES) for t in range(tiles)]
+
+    def regroup(first, refs, t):
+        cut = slice(t * LANES, t * LANES + span[t])
+        for k, source in enumerate(refs):
+            stage[first + k, t, :, : span[t]] = source[:, cut].astype(F32)
+        for r in range(R):
+            yield r, cut, [
+                stage[first + k, t, pl.ds(r, SUB, stride=R), :][:, : span[t]] for k in range(len(refs))
+            ]
+
+    for copy in loads[:2]:
         copy.wait()
-
-    span = [min(LANES, nrows - t * LANES) for t in range(tiles)]
-    sources = (
-        mask_ref, conc_ref, class_ref, s_ref.at[0], s_ref.at[1], s_ref.at[2], e_ref.at[0], e_ref.at[1], e_ref.at[2]
-    )
     count = jnp.zeros((SUB, LANES), F32)
     for t in range(tiles):
-        cut = slice(t * LANES, t * LANES + span[t])
-        for k, source in enumerate(sources):
-            stage[k, t, :, : span[t]] = source[:, cut].astype(F32)
-        for r in range(R):
-            oc, conc, grade, s1, s2, s3, one, two, shear = (
-                stage[k, t, pl.ds(r, SUB, stride=R), :][:, : span[t]] for k in range(9)
-            )
+        for r, cut, (oc, conc) in regroup(0, (mask_ref, conc_ref), t):
             ocean[r, :, cut] = oc
+            orl[r, :, cut] = oc / (0.6 * conc)
             base[r, :, cut] = conc * jnp.exp(-2.0 * (1.0 - conc))
-            orl[r, :, cut] = oc / (0.6 * conc)
-            Z[0, r, :, cut] = oc * 0.1 * grade * conc
+            Z[0, r, :, cut] = oc * 0.1 * conc
+    for m in range(width):
+        fixed_out[0, 0, m : m + 1, :] = orl[R - width + m, SUB - 1 : SUB, :]
+        fixed_out[0, 1, m : m + 1, :] = ocean[R - width + m, SUB - 1 : SUB, :]
+        fixed_out[1, 0, m : m + 1, :] = orl[width - 1 - m, 0:1, :]
+        fixed_out[1, 1, m : m + 1, :] = ocean[width - 1 - m, 0:1, :]
+
+    def fixed_copy(k, to):
+        return pltpu.make_async_remote_copy(
+            src_ref=fixed_out.at[k, :, pl.ds(0, width), :], dst_ref=fixed_in.at[k, :, pl.ds(0, width), :],
+            send_sem=fixed_send, recv_sem=fixed_recv, device_id=dev(to, lat), device_id_type=MESH,
+        )
+
+    def far_first(up, down):
+        odd = lax.rem(lon, 2) == 1
+
+        @pl.when(odd)
+        def _():
+            up()
+            down()
+
+        @pl.when(jnp.logical_not(odd))
+        def _():
+            down()
+            up()
+
+    for copy in loads[2:5]:
+        copy.wait()
+    sources = (class_ref, s_ref.at[0], s_ref.at[1], s_ref.at[2], e_ref.at[0], e_ref.at[1], e_ref.at[2])
+    for t in range(tiles):
+        for r, cut, (grade, s1, s2, s3, one, two, shear) in regroup(2, sources, t):
+            oc = ocean[r, :, cut]
+            Z[0, r, :, cut] = Z[0, r, :, cut] * grade
             for k, part in enumerate((s1, s2, s3)):
                 state[k, r, :, cut] = oc * part
             load[0, r, :, cut] = (one + two / 3.0) / (8.0 / 9.0)
             load[1, r, :, cut] = (two + one / 3.0) / (8.0 / 9.0)
             load[2, r, :, cut] = (shear / (4.0 / 3.0)) / (8.0 / 9.0)
-    for m in range(width):
-        fixed_out[0, 0, m : m + 1, :] = orl[R - width + m, SUB - 1 : SUB, :]
-        fixed_out[0, 1, m : m + 1, :] = ocean[R - width + m, SUB - 1 : SUB, :]
-        fixed_out[1, 0, m : m + 1, :] = orl[width - 1 - m, 0:1, :]
-        fixed_out[1, 1, m : m + 1, :] = ocean[width - 1 - m, 0:1, :]
     for r in range(R):
         oc = ocean[r]
         Z[8, r] = oc
@@ -137,28 +164,7 @@
         for t in range(tiles):
             count = count + tile(oc, t)
     count = jnp.sum(count, axis=0, keepdims=True)
-
     pl.semaphore_wait(barrier, n - 1)
-
-    def fixed_copy(k, to):
-        return pltpu.make_async_remote_copy(
-            src_ref=fixed_out.at[k, :, pl.ds(0, width), :], dst_ref=fixed_in.at[k, :, pl.ds(0, width), :],
-            send_sem=fixed_send, recv_sem=fixed_recv, device_id=dev(to, lat), device_id_type=MESH,
-        )
-
-    def far_first(up, down):
-        odd = lax.rem(lon, 2) == 1
-
-        @pl.when(odd)
-        def _():
-            up()
-            down()
-
-        @pl.when(jnp.logical_not(odd))
-        def _():
-            down()
-            up()
-
     far_first(lambda: fixed_copy(0, right).start(), lambda: fixed_copy(1, left).start())
 
     def conv(f, c):
@@ -240,7 +246,7 @@
             Z[4, r] = keep * q
             for k in range(3):
                 Z[1 + k, r] = el[k]
-                Z[5 + k, r] = -(el[k] * q)
+                Z[5 + k, r] = el[k] * q
             for m in range(width):
                 for f, part in enumerate((damage, *el)):
                     for t in range(tiles):
@@ -257,7 +263,19 @@
                 recv_sem=stat_recv.at[it], device_id=peer(d), device_id_type=MESH,
             )
 
+        def row_copy(s, m, to):
+            piece = pl.ds(SUB * m + 4 * s, 4)
+            return pltpu.make_async_remote_copy(
+                src_ref=rows_out.at[it, :, piece, :], dst_ref=rows_in.at[it, :, piece, :], send_sem=row_send,
+                recv_sem=row_recv.at[it], device_id=dev(to, lat), device_id_type=MESH,
+            )
+
+        def start_rows(s, to, ms):
+            for m in ms:
+                row_copy(s, m, to).start()
+
         every(1, n, lambda d: stat_copy(d).start())
+        far_first(lambda: start_rows(0, right, [0]), lambda: start_rows(1, left, [0]))
 
         low = jnp.zeros((SUB, LANES), F32)
         high = jnp.zeros((SUB, LANES), F32)
@@ -292,26 +310,15 @@
         for k in range(3):
             lat_copy(k).start()
 
-        def row_copy(s, m, to):
-            piece = pl.ds(SUB * m + 4 * s, 4)
-            return pltpu.make_async_remote_copy(
-                src_ref=rows_out.at[it, :, piece, :], dst_ref=rows_in.at[it, :, piece, :], send_sem=row_send,
-                recv_sem=row_recv.at[it], device_id=dev(to, lat), device_id_type=MESH,
-            )
-
-        def start_rows(s, to):
-            for m in range(width):
-                row_copy(s, m, to).start()
-
-        far_first(lambda: start_rows(0, right), lambda: start_rows(1, left))
+        rest = list(range(1, width))
+        far_first(lambda: start_rows(0, right, rest), lambda: start_rows(1, left, rest))
 
         lax.fori_loop(0, jnp.where(it == 0, 9, 8), conv, 0)
 
         def drain(ref, sem):
             pltpu.make_async_copy(ref, ref, sem).wait()
 
-        def wait_halos():
-            drain(rows_in.at[it, :, pl.ds(0, SUB * width), :], row_recv.at[it])
+        def wait_slabs():
             drain(lat_in.at[it], lat_recv.at[it])
 
             @pl.when(is_last)
@@ -331,11 +338,13 @@
         mean_ref[...] = jnp.where(lane == it, mean, mean_ref[...])
 
         def columns():
+            signed = jnp.where(lax.rem(lane, 32) < width, factor, -factor)
+
             @pl.when(is_last)
             def _():
                 def spread(k):
                     got = fold_in[it, k]
-                    got = got + factor * pltpu.roll(got, LANES - 16, 1)
+                    got = got + signed * pltpu.roll(got, LANES - 16, 1)
                     for r in range(R):
                         tops[pl.ds((k * R + r) * SUB, SUB), :] = pltpu.roll(got, (NORTH - 32 * r) % LANES, 1)
 
@@ -347,7 +356,7 @@
             own = []
             for k in range(3):
                 got = lat_in[it, k]
-                got = got + factor * pltpu.roll(got, LANES - 16, 1)
+                got = got + signed * pltpu.roll(got, LANES - 16, 1)
                 own.append(jnp.where(is_last, got, flip(got, packed_slot)))
 
             def piece(k, r):
@@ -420,7 +429,7 @@
 
         @pl.when(it == 0)
         def _():
-            wait_halos()
+            wait_slabs()
             columns()
             finish_ocean()
 
@@ -429,8 +438,9 @@
                 cut = slice(t * LANES, (t + 1) * LANES)
                 ho, hr = half_ocean[r, :, cut], half_rden[r, :, cut]
                 for f in range(4):
-                    local = Z[f, r, :, cut] + factor * Z[4 + f, r, :, cut]
-                    spread_out = Y[f, r, :, cut] + factor * Y[4 + f, r, :, cut]
+                    part = factor if f == 0 else -factor
+                    local = Z[f, r, :, cut] + part * Z[4 + f, r, :, cut]
+                    spread_out = Y[f, r, :, cut] + part * Y[4 + f, r, :, cut]
                     fresh = ho * local + hr * spread_out
                     if f == 0:
                         Z[0, r, :, cut] = fresh
@@ -439,9 +449,18 @@
 
         @pl.when(it > 0)
         def _():
-            wait_halos()
+            wait_slabs()
             columns()
 
+        for f in range(4):
+            for r in range(R):
+                into = Z.at[0, r] if f == 0 else state.at[f - 1, r]
+                south, north = column_term(f, r)
+                for t, term in ((0, south), (tiles - 1, north)):
+                    cut = slice(t * LANES, (t + 1) * LANES)
+                    into[:, cut] = into[:, cut] + half_rden[r, :, cut] * term
+
+        drain(rows_in.at[it, :, pl.ds(0, SUB * width), :], row_recv.at[it])
         for t in range(tiles):
             e = [rows_in[it, t, pl.ds(k, SUB, stride=4), :] for k in range(1, 4)]
             half = (e[0] - e[1]) * 0.5
@@ -460,15 +479,9 @@
         for f in range(4):
             for r in range(R):
                 into = Z.at[0, r] if f == 0 else state.at[f - 1, r]
-                south, north = column_term(f, r)
                 for t in range(tiles):
                     cut = slice(t * LANES, (t + 1) * LANES)
-                    add = row_term(r, f, t)
-                    if t == 0:
-                        add = add + half_rden[r, :, cut] * south
-                    if t == tiles - 1:
-                        add = add + half_rden[r, :, cut] * north
-                    into[:, cut] = into[:, cut] + add
+                    into[:, cut] = into[:, cut] + row_term(r, f, t)
 
         drain(stat_in.at[it, pl.ds(1, n - 1)], stat_send)
         drain(rows_out.at[it], row_send)
@@ -560,7 +573,7 @@
         in_specs=[vmem] * 3,
         out_specs=(hbm,) * 3,
         scratch_shapes=[pltpu.SMEM((ITERS,), F32), S(3)],
-    )(stress, damage, mean)
+    )(*(pltpu.with_memory_space_constraint(x, pltpu.VMEM) for x in (stress, damage, mean)))
 
 
 def solution(mesh):

time: 31.2 us -> 28.2 us (0.904)
  local copies, waits for them, and re-layouts: 1.99 us -> 0 us
  Pallas kernels: 28.2 us -> 27.4 us
    unnamed x6 -> x0, local copies, waits for them, and re-layouts: 1.99 us -> none
    pallas_call x1, Pallas kernels: 1.93 us -> 0.84 us  [shards(): pl.pallas_call(write_out, out_shape=(jax.ShapeDtypeStruct((3, ncols, nrow...]
where the time goes in v1:
time: 28.2 us; the launch traced here: 28.1 us
  Pallas kernels  27.4 us (97%)
  between operations  0.64 us (2%)
    pallas_call x1, Pallas kernels, shards(): pl.pallas_call(functools.partial(kernel, nlon, nlat, nrows, R, L, side),...  26.6 us
    pallas_call x1, Pallas kernels, shards(): pl.pallas_call(write_out, out_shape=(jax.ShapeDtypeStruct((3, ncols, nrow...  0.84 us

profile of v1, /device:TPU:1, one launch (start us, length us, event | category | flops | bytes accessed | tf_op | source)
XLA Modules:
  0.0 28.1 jit_solution(15625204370799872434)
XLA Ops:
  0.6 26.6 %shard_map.94 = (f32[3,32,1080]{2,1,0:T(8,128)S(1)}, f32[32,1080]{1,0:T(8,128)S(1)}, f32[8,128]{1,0:T(8,128)S(1)}) custom-call(f32[7,7]{1,0:T(8,128)} %w_hbm.1, s32[256]{0:T(256)} %partner_hbm.1, f32[3,32,1080]{2,1,0:T(8,128)} %e_hbm.1, f32[3,32,1080]{2,1,0:T(8,128)} %s_hbm.1, f32[32,1080]{1,0:T(8,128)} %conc_hbm.1, s32[32,1080]{1,0:T(8,128)} %class_hbm.1, ...), custom_call_target="tpu_custom_call" | custom-call | tf_op jit(solution)/shard_map/pallas_call | solution.py:537
  27.2 0.8 %shard_map.95 = (f32[3,32,1080]{2,1,0:T(8,128)}, f32[32,1080]{1,0:T(8,128)}, f32[3]{0:T(128)}) custom-call(f32[3,32,1080]{2,1,0:T(8,128)S(1)} %get-tuple-element.6.stress_vmem, f32[32,1080]{1,0:T(8,128)S(1)} %get-tuple-element.7.damage_vmem, f32[8,128]{1,0:T(8,128)S(1)} %get-tuple-element.8.mean_vmem), custom_call_target="tpu_custom_call" | custom-call | tf_op jit(solution)/shard_map/pallas_call | solution.py:566

commit v2 on v1

--- a/solution.py
+++ b/solution.py
@@ -20,7 +20,7 @@
     w_hbm, partner_hbm, e_hbm, s_hbm, conc_hbm, class_hbm, mask_hbm,
     stress_ref, damage_ref, mean_ref,
     w_ref, partner_ref, where_ref,
-    Z, Y, X, load, base, ocean, orl, half_ocean, half_rden, state,
+    Z, Y, XH, XL, TH, TL, load, base, ocean, orl, half_ocean, half_rden, state,
     rows_out, rows_in, fixed_out, fixed_in, fixed_rows, HQ, WR, WC, C, rden_rows,
     slab, lat_in, fold_in, tops, D, T, stat, stat_in, stage,
     e_ref, s_ref, conc_ref, class_ref, mask_ref,
@@ -160,6 +160,7 @@
     for r in range(R):
         oc = ocean[r]
         Z[8, r] = oc
+        Z[9, r] = jnp.zeros((SUB, L), F32)
         half_ocean[r] = 0.5 * oc
         for t in range(tiles):
             count = count + tile(oc, t)
@@ -167,27 +168,79 @@
     pl.semaphore_wait(barrier, n - 1)
     far_first(lambda: fixed_copy(0, right).start(), lambda: fixed_copy(1, left).start())
 
-    def conv(f, c):
+    pairs = (R + 2 * width) // 2
+    taps = (side + 1) // 2
+    step = LANES - 2 * width
+    block = 2 * tiles * SUB
+
+    def build_bands():
+        for strip in range(LANES // 16):
+            row = lax.broadcasted_iota(jnp.int32, (16, LANES), 0)
+            offset = row + 16 * strip + width - lax.broadcasted_iota(jnp.int32, (16, LANES), 1)
+            hits = [offset == b for b in range(side)]
+            for a in range(-1, side + 1):
+                band = jnp.zeros((16, LANES), F32)
+                if 0 <= a < side:
+                    for b in range(side):
+                        band = jnp.where(hits[b], w_ref[a, b], band)
+                high = band.astype(jnp.bfloat16)
+                low = (band - high.astype(F32)).astype(jnp.bfloat16)
+                for k in range(taps):
+                    for u in range(2):
+                        for v in range(2):
+                            if 2 * k + u - v == a:
+                                at = (slice(k * 256 + u * LANES + 16 * strip, k * 256 + u * LANES + 16 * strip + 16),
+                                      slice(v * LANES, (v + 1) * LANES))
+                                TH[at] = high
+                                TL[at] = low
+
+    def conv(g, c):
+        chunks = []
         for r in range(R):
-            X[width + r] = Z[f, r]
-        for m in range(width):
-            X[m] = jnp.where(sub_wide == 0, 0.0, pltpu.roll(Z[f, m + R - width], 1, 0))
-            X[R + width + m] = jnp.where(sub_wide == SUB - 1, 0.0, pltpu.roll(Z[f, m], SUB - 1, 0))
-        for b in range(side):
-            acc = [None] * R
-            for p in range(R + 2 * width):
-                x = X[p]
-                for r in range(R):
-                    a = p - r
-                    if 0 <= a < side:
-                        term = w_ref[a, b] * x
-                        acc[r] = term if acc[r] is None else acc[r] + term
-            for r in range(R):
-                moved = acc[r] if b == width else pltpu.roll(acc[r], (width - b) % L, 1)
-                if b == 0:
-                    Y[f, r] = moved
-                else:
-                    Y[f, r] = Y[f, r] + moved
+            plane = []
+            for i in range(2):
+                last = None
+                for t in range(tiles):
+                    shift = width + (LANES - step) * t
+                    here = Z[2 * g + i, r, :, t * LANES : (t + 1) * LANES]
+                    now = pltpu.roll(here, shift, 1)
+                    before = 0.0 if last is None else pltpu.roll(last, shift, 1)
+                    plane.append(jnp.where(lane < shift, before, now))
+                    last = here
+            chunks.append(plane)
+        for p in range(R + 2 * width):
+            if p < width:
+                plane = [jnp.where(sub == 0, 0.0, pltpu.roll(x, 1, 0)) for x in chunks[p + R - width]]
+            elif p < width + R:
+                plane = chunks[p - width]
+            else:
+                plane = [jnp.where(sub == SUB - 1, 0.0, pltpu.roll(x, SUB - 1, 0)) for x in chunks[p - width - R]]
+            for j in range(tiles):
+                x = jnp.concatenate(plane[2 * j : 2 * j + 2], axis=0)
+                high = x.astype(jnp.bfloat16)
+                at = (slice((p // 2) * block + 16 * j, (p // 2) * block + 16 * j + 16),
+                      slice((p % 2) * LANES, (p % 2 + 1) * LANES))
+                XH[at] = high
+                XL[at] = (x - high.astype(F32)).astype(jnp.bfloat16)
+        out = None
+        for k in range(taps):
+            rows = slice(k * block, k * block + (R // 2) * block)
+            band = slice(k * 256, (k + 1) * 256)
+            for x, w in ((XH, TH), (XL, TH), (XH, TL)):
+                term = jnp.dot(x[rows, :], w[band, :], preferred_element_type=F32)
+                out = term if out is None else out + term
+        for r in range(R):
+            for i in range(2):
+                def part(t):
+                    row = (r // 2) * block + (i * tiles + t) * SUB
+                    return out[row : row + SUB, (r % 2) * LANES : (r % 2 + 1) * LANES]
+                for t in range(tiles):
+                    first = width + (LANES - step) * t
+                    value = pltpu.roll(part(t), LANES - first, 1)
+                    if t + 1 < tiles:
+                        rest = pltpu.roll(part(t + 1), LANES - width - first - width, 1)
+                        value = jnp.where(lane < LANES - width - first, value, rest)
+                    Y[2 * g + i, r, :, t * LANES : (t + 1) * LANES] = value
         return c
 
     def row_terms(halos):
@@ -313,7 +366,11 @@
         rest = list(range(1, width))
         far_first(lambda: start_rows(0, right, rest), lambda: start_rows(1, left, rest))
 
-        lax.fori_loop(0, jnp.where(it == 0, 9, 8), conv, 0)
+        @pl.when(it == 0)
+        def _():
+            build_bands()
+
+        lax.fori_loop(0, jnp.where(it == 0, 5, 4), conv, 0)
 
         def drain(ref, sem):
             pltpu.make_async_copy(ref, ref, sem).wait()
@@ -529,6 +586,7 @@
     tiles = L // LANES
     n = nlon * nlat
     V = lambda *shape: pltpu.VMEM(shape, F32)
+    B = lambda *shape: pltpu.VMEM(shape, jnp.bfloat16)
     S = lambda *shape: pltpu.SemaphoreType.DMA(shape)
     planes = R + 2 * width
     ext = -(-(ncols + 2 * width) // SUB) * SUB
@@ -546,7 +604,8 @@
         scratch_shapes=[
             pltpu.SMEM(kernel_weights.shape, F32), pltpu.SMEM(fold_partner.shape, jnp.int32),
             pltpu.SMEM((ncols + 2 * width,), jnp.int32),
-            V(9, R, SUB, L), V(9, R, SUB, L), V(planes, SUB, L),
+            V(10, R, SUB, L), V(10, R, SUB, L), B(planes * tiles * SUB, 256), B(planes * tiles * SUB, 256),
+            B((side + 1) * LANES, 256), B((side + 1) * LANES, 256),
             V(3, R, SUB, L), V(R, SUB, L), V(R, SUB, L), V(R, SUB, L), V(R, SUB, L), V(R, SUB, L), V(3, R, SUB, L),
             V(ITERS, tiles, SUB * width, LANES), V(ITERS, tiles, SUB * (width + 1), LANES),
             V(2, 2, 4, L), V(2, 2, 4, L), V(tiles, SUB, LANES), V(tiles, SUB, LANES),

time: 28.2 us -> 26.2 us (0.929)
  Pallas kernels: 27.4 us -> 25.2 us
    pallas_call x1, Pallas kernels: 26.6 us -> 24.4 us  [shards(): pl.pallas_call(functools.partial(kernel, nlon, nlat, nrows, R, L, side),...]
where the time goes in v2:
time: 26.2 us; the launch traced here: 25.9 us
  Pallas kernels  25.2 us (96%)
  between operations  0.64 us (2%)
    pallas_call x1, Pallas kernels, shards(): pl.pallas_call(functools.partial(kernel, nlon, nlat, nrows, R, L, side),...  24.4 us
    pallas_call x1, Pallas kernels, shards(): pl.pallas_call(write_out, out_shape=(jax.ShapeDtypeStruct((3, ncols, nrow...  0.84 us

profile of v2, /device:TPU:1, one launch (start us, length us, event | category | flops | bytes accessed | tf_op | source)
XLA Modules:
  0.0 25.9 jit_solution(898114237311489966)
XLA Ops:
  0.6 24.4 %shard_map.94 = (f32[3,32,1080]{2,1,0:T(8,128)S(1)}, f32[32,1080]{1,0:T(8,128)S(1)}, f32[8,128]{1,0:T(8,128)S(1)}) custom-call(f32[7,7]{1,0:T(8,128)} %w_hbm.1, s32[256]{0:T(256)} %partner_hbm.1, f32[3,32,1080]{2,1,0:T(8,128)} %e_hbm.1, f32[3,32,1080]{2,1,0:T(8,128)} %s_hbm.1, f32[32,1080]{1,0:T(8,128)} %conc_hbm.1, s32[32,1080]{1,0:T(8,128)} %class_hbm.1, ...), custom_call_target="tpu_custom_call" | custom-call | tf_op jit(solution)/shard_map/pallas_call | solution.py:595
  25.0 0.8 %shard_map.95 = (f32[3,32,1080]{2,1,0:T(8,128)}, f32[32,1080]{1,0:T(8,128)}, f32[3]{0:T(128)}) custom-call(f32[3,32,1080]{2,1,0:T(8,128)S(1)} %get-tuple-element.6.stress_vmem, f32[32,1080]{1,0:T(8,128)S(1)} %get-tuple-element.7.damage_vmem, f32[8,128]{1,0:T(8,128)S(1)} %get-tuple-element.8.mean_vmem), custom_call_target="tpu_custom_call" | custom-call | tf_op jit(solution)/shard_map/pallas_call | solution.py:625

commit v3 on v2

--- a/solution.py
+++ b/solution.py
@@ -84,22 +84,6 @@
             rows_in[it, t, SUB * width :, :] = edge
         fixed_rows[t] = edge
     mean_ref[...] = edge
-    for copy in loads[5:]:
-        copy.wait()
-    for d in range(width):
-        for b in range(side):
-            WR[d * side + b] = jnp.where(sub < 4, w_ref[d, b], w_ref[side - 1 - d, b])
-    span_lanes = 5 * width
-    for d in range(1, width + 1):
-        keep = (slot >= width - d) & ((lane < span_lanes) | ((lane >= NORTH) & (lane < NORTH + span_lanes)))
-        for a in range(side):
-            WC[(d - 1) * side + a] = jnp.where(
-                keep, jnp.where(lane < NORTH - width, w_ref[a, width - d], w_ref[a, width + d]), 0.0
-            )
-    for i in range(ncols + 2 * width):
-        p = partner_ref[lax.rem(lon * ncols + i - width + nlon * ncols, nlon * ncols)]
-        col = lax.rem(p, ncols)
-        where_ref[i] = ((p // ncols) * R + lax.rem(col, R)) * SUB + col // R
     span = [min(LANES, nrows - t * LANES) for t in range(tiles)]
 
     def regroup(first, refs, t):
@@ -145,18 +129,14 @@
             down()
             up()
 
-    for copy in loads[2:5]:
+    for copy in loads[2:4]:
         copy.wait()
-    sources = (class_ref, s_ref.at[0], s_ref.at[1], s_ref.at[2], e_ref.at[0], e_ref.at[1], e_ref.at[2])
     for t in range(tiles):
-        for r, cut, (grade, s1, s2, s3, one, two, shear) in regroup(2, sources, t):
+        for r, cut, (grade, s1, s2, s3) in regroup(2, (class_ref, s_ref.at[0], s_ref.at[1], s_ref.at[2]), t):
             oc = ocean[r, :, cut]
             Z[0, r, :, cut] = Z[0, r, :, cut] * grade
             for k, part in enumerate((s1, s2, s3)):
                 state[k, r, :, cut] = oc * part
-            load[0, r, :, cut] = (one + two / 3.0) / (8.0 / 9.0)
-            load[1, r, :, cut] = (two + one / 3.0) / (8.0 / 9.0)
-            load[2, r, :, cut] = (shear / (4.0 / 3.0)) / (8.0 / 9.0)
     for r in range(R):
         oc = ocean[r]
         Z[8, r] = oc
@@ -164,9 +144,33 @@
         half_ocean[r] = 0.5 * oc
         for t in range(tiles):
             count = count + tile(oc, t)
+    loads[4].wait()
+    for t in range(tiles):
+        for r, cut, (one, two, shear) in regroup(6, (e_ref.at[0], e_ref.at[1], e_ref.at[2]), t):
+            load[0, r, :, cut] = (one + two / 3.0) / (8.0 / 9.0)
+            load[1, r, :, cut] = (two + one / 3.0) / (8.0 / 9.0)
+            load[2, r, :, cut] = (shear / (4.0 / 3.0)) / (8.0 / 9.0)
     count = jnp.sum(count, axis=0, keepdims=True)
     pl.semaphore_wait(barrier, n - 1)
     far_first(lambda: fixed_copy(0, right).start(), lambda: fixed_copy(1, left).start())
+
+    def build_tables():
+        for copy in loads[5:]:
+            copy.wait()
+        for d in range(width):
+            for b in range(side):
+                WR[d * side + b] = jnp.where(sub < 4, w_ref[d, b], w_ref[side - 1 - d, b])
+        span_lanes = 5 * width
+        for d in range(1, width + 1):
+            keep = (slot >= width - d) & ((lane < span_lanes) | ((lane >= NORTH) & (lane < NORTH + span_lanes)))
+            for a in range(side):
+                WC[(d - 1) * side + a] = jnp.where(
+                    keep, jnp.where(lane < NORTH - width, w_ref[a, width - d], w_ref[a, width + d]), 0.0
+                )
+        for i in range(ncols + 2 * width):
+            p = partner_ref[lax.rem(lon * ncols + i - width + nlon * ncols, nlon * ncols)]
+            col = lax.rem(p, ncols)
+            where_ref[i] = ((p // ncols) * R + lax.rem(col, R)) * SUB + col // R
 
     pairs = (R + 2 * width) // 2
     taps = (side + 1) // 2
@@ -194,7 +198,7 @@
                                 TH[at] = high
                                 TL[at] = low
 
-    def conv(g, c):
+    def build(g, buf):
         chunks = []
         for r in range(R):
             plane = []
@@ -220,14 +224,16 @@
                 high = x.astype(jnp.bfloat16)
                 at = (slice((p // 2) * block + 16 * j, (p // 2) * block + 16 * j + 16),
                       slice((p % 2) * LANES, (p % 2 + 1) * LANES))
-                XH[at] = high
-                XL[at] = (x - high.astype(F32)).astype(jnp.bfloat16)
+                XH[(buf, *at)] = high
+                XL[(buf, *at)] = (x - high.astype(F32)).astype(jnp.bfloat16)
+
+    def multiply(g, buf):
         out = None
         for k in range(taps):
             rows = slice(k * block, k * block + (R // 2) * block)
             band = slice(k * 256, (k + 1) * 256)
             for x, w in ((XH, TH), (XL, TH), (XH, TL)):
-                term = jnp.dot(x[rows, :], w[band, :], preferred_element_type=F32)
+                term = jnp.dot(x[buf, rows, :], w[band, :], preferred_element_type=F32)
                 out = term if out is None else out + term
         for r in range(R):
             for i in range(2):
@@ -241,7 +247,6 @@
                         rest = pltpu.roll(part(t + 1), LANES - width - first - width, 1)
                         value = jnp.where(lane < LANES - width - first, value, rest)
                     Y[2 * g + i, r, :, t * LANES : (t + 1) * LANES] = value
-        return c
 
     def row_terms(halos):
         for r in range(width):
@@ -291,7 +296,8 @@
             bk = base[r] * keep
             el = [scale * (state[k, r] + bk * load[k, r]) for k in range(3)]
             half = (el[0] - el[1]) * 0.5
-            tau = jnp.sqrt(half * half + el[2] * el[2] + 0.25)
+            tau = half * half + el[2] * el[2] + 0.25
+            tau = tau * lax.rsqrt(tau)
             over = jnp.maximum((tau + 0.35 * (el[0] + el[1])) * orl[r], 1.0)
             q = 1.0 - 1.0 / over
             for t in range(tiles):
@@ -368,9 +374,16 @@
 
         @pl.when(it == 0)
         def _():
+            build_tables()
             build_bands()
-
-        lax.fori_loop(0, jnp.where(it == 0, 5, 4), conv, 0)
+            build(4, 1)
+            multiply(4, 1)
+
+        build(0, 0)
+        for g in range(4):
+            if g + 1 < 4:
+                build(g + 1, (g + 1) % 2)
+            multiply(g, g % 2)
 
         def drain(ref, sem):
             pltpu.make_async_copy(ref, ref, sem).wait()
@@ -381,6 +394,18 @@
             @pl.when(is_last)
             def _():
                 drain(fold_in.at[it, pl.ds(0, nlon - 1)], fold_recv.at[it])
+
+        def fold_in_place():
+            for r in range(R):
+                for t in range(tiles):
+                    cut = slice(t * LANES, (t + 1) * LANES)
+                    ho, hr = half_ocean[r, :, cut], half_rden[r, :, cut]
+                    for f in range(8):
+                        Y[f, r, :, cut] = ho * Z[f, r, :, cut] + hr * Y[f, r, :, cut]
+
+        @pl.when(it > 0)
+        def _():
+            fold_in_place()
 
         drain(stat_in.at[it, pl.ds(1, n - 1)], stat_recv.at[it])
         total = stat[it]
@@ -489,16 +514,14 @@
             wait_slabs()
             columns()
             finish_ocean()
+            fold_in_place()
 
         for r in range(R):
             for t in range(tiles):
                 cut = slice(t * LANES, (t + 1) * LANES)
-                ho, hr = half_ocean[r, :, cut], half_rden[r, :, cut]
                 for f in range(4):
                     part = factor if f == 0 else -factor
-                    local = Z[f, r, :, cut] + part * Z[4 + f, r, :, cut]
-                    spread_out = Y[f, r, :, cut] + part * Y[4 + f, r, :, cut]
-                    fresh = ho * local + hr * spread_out
+                    fresh = Y[f, r, :, cut] + part * Y[4 + f, r, :, cut]
                     if f == 0:
                         Z[0, r, :, cut] = fresh
                     else:
@@ -521,7 +544,8 @@
         for t in range(tiles):
             e = [rows_in[it, t, pl.ds(k, SUB, stride=4), :] for k in range(1, 4)]
             half = (e[0] - e[1]) * 0.5
-            tau = jnp.sqrt(half * half + e[2] * e[2] + 0.25)
+            tau = half * half + e[2] * e[2] + 0.25
+            tau = tau * lax.rsqrt(tau)
             over = jnp.maximum((tau + 0.35 * (e[0] + e[1])) * fixed_rows[t], 1.0)
             HQ[t] = factor * (1.0 - 1.0 / over)
         halos = [[None] * tiles for _ in range(width)]
@@ -604,7 +628,7 @@
         scratch_shapes=[
             pltpu.SMEM(kernel_weights.shape, F32), pltpu.SMEM(fold_partner.shape, jnp.int32),
             pltpu.SMEM((ncols + 2 * width,), jnp.int32),
-            V(10, R, SUB, L), V(10, R, SUB, L), B(planes * tiles * SUB, 256), B(planes * tiles * SUB, 256),
+            V(10, R, SUB, L), V(10, R, SUB, L), B(2, planes * tiles * SUB, 256), B(2, planes * tiles * SUB, 256),
             B((side + 1) * LANES, 256), B((side + 1) * LANES, 256),
             V(3, R, SUB, L), V(R, SUB, L), V(R, SUB, L), V(R, SUB, L), V(R, SUB, L), V(R, SUB, L), V(3, R, SUB, L),
             V(ITERS, tiles, SUB * width, LANES), V(ITERS, tiles, SUB * (width + 1), LANES),

time: 26.2 us -> 26.2 us (level)
  no operation moved by 1% of the time
where the time goes in v3:
time: 26.2 us; the launch traced here: 25.8 us
  Pallas kernels  25.1 us (96%)
  between operations  0.64 us (2%)
    pallas_call x1, Pallas kernels, shards(): pl.pallas_call(functools.partial(kernel, nlon, nlat, nrows, R, L, side),...  24.3 us
    pallas_call x1, Pallas kernels, shards(): pl.pallas_call(write_out, out_shape=(jax.ShapeDtypeStruct((3, ncols, nrow...  0.84 us

profile of v3, /device:TPU:1, one launch (start us, length us, event | category | flops | bytes accessed | tf_op | source)
XLA Modules:
  0.0 25.8 jit_solution(5600591088756984226)
XLA Ops:
  0.6 24.3 %shard_map.94 = (f32[3,32,1080]{2,1,0:T(8,128)S(1)}, f32[32,1080]{1,0:T(8,128)S(1)}, f32[8,128]{1,0:T(8,128)S(1)}) custom-call(f32[7,7]{1,0:T(8,128)} %w_hbm.1, s32[256]{0:T(256)} %partner_hbm.1, f32[3,32,1080]{2,1,0:T(8,128)} %e_hbm.1, f32[3,32,1080]{2,1,0:T(8,128)} %s_hbm.1, f32[32,1080]{1,0:T(8,128)} %conc_hbm.1, s32[32,1080]{1,0:T(8,128)} %class_hbm.1, ...), custom_call_target="tpu_custom_call" | custom-call | tf_op jit(solution)/shard_map/pallas_call | solution.py:619
  24.9 0.8 %shard_map.95 = (f32[3,32,1080]{2,1,0:T(8,128)}, f32[32,1080]{1,0:T(8,128)}, f32[3]{0:T(128)}) custom-call(f32[3,32,1080]{2,1,0:T(8,128)S(1)} %get-tuple-element.6.stress_vmem, f32[32,1080]{1,0:T(8,128)S(1)} %get-tuple-element.7.damage_vmem, f32[8,128]{1,0:T(8,128)S(1)} %get-tuple-element.8.mean_vmem), custom_call_target="tpu_custom_call" | custom-call | tf_op jit(solution)/shard_map/pallas_call | solution.py:649
